TPU v7x, 32 devices: a whole 2x2x4 slice. The times are simulated.
32 devices in a mesh: reg: 4 (over y, core), prod: 8 (over z, x).
Axes of the slice: x: 2, y: 2, z: 4, core: 2. Of those that a mesh axis runs over, the one named last changes fastest.
Arguments:
- bottom_series_predictions: float32 [128, 256, 128], P('reg', 'prod'), may hold values from -6 to 6
- group_item_predictions: float32 [32, 256, 128], P('reg', 'prod'), may hold values from -18 to 18
- area_class_predictions: float32 [128, 32, 128], P('reg', 'prod'), may hold values from -18 to 18
- group_class_predictions: float32 [32, 32, 128], P('reg'), may hold values from -48 to 48
- bottom_series_precision: float32 [128, 256], P('reg', 'prod'), may hold values from 0.5 to 5
- group_item_precision: float32 [32, 256], P('reg', 'prod'), may hold values from 0.02 to 0.5
- area_class_precision: float32 [128, 32], P('reg', 'prod'), may hold values from 0.02 to 0.5
- group_class_precision: float32 [32, 32], P('reg'), may hold values from 0.002 to 0.05
- group_area_partition: int32 [32, 128], replicated, may hold values from -1 to 127, as said below
- class_item_partition: int32 [32, 128], replicated, may hold values from -1 to 255, as said below
Outputs:
- solution_field: float32 [128, 256, 128], P('reg', 'prod')
- residual: float32 [128, 256, 128], P('reg', 'prod')
Inputs may be any that keep to these rules, and one draw needn't show every extreme that they name: `group_area_partition`: every region stands in exactly one row; each row holds its parent's regions in its first slots and -1 in the rest; a parent has 1 to 97 regions, and some parent has exactly 97. `class_item_partition`: every product stands in exactly one row; each row holds its category's products in its first slots and -1 in the rest; a category has 1 to 128 products, and some category has exactly 128.
All inputs are finite; a program needn't handle non-finite values.
Results may differ from a plain program's by a relative error of at most 0.00011.
Values sent between devices are 32-bit elements; how exact they have to be, the bound alone decides.
A program may use at most 64 MiB of HBM per device.

v0:
```python
import jax
import jax.numpy as jnp
from jax import lax
from jax.sharding import PartitionSpec as P

ITERATIONS = 2


def member_local(table, first, count):
    items = first + jnp.arange(count, dtype=jnp.int32)
    return jnp.any(table[:, :, None] == items[None, None, :], axis=1).astype(jnp.float32)


def on_device(
    bottom_series_predictions,
    group_item_predictions,
    area_class_predictions,
    group_class_predictions,
    bottom_series_precision,
    group_item_precision,
    area_class_precision,
    group_class_precision,
    group_area_partition,
    class_item_partition,
):
    high = lax.Precision.HIGHEST
    areas_overall, items_overall, horizon_length = bottom_series_predictions.shape
    area_index_table = member_local(
        group_area_partition, lax.axis_index("reg") * areas_overall, areas_overall
    )
    item_index_table = member_local(
        class_item_partition, lax.axis_index("prod") * items_overall, items_overall
    )
    parent_share = area_index_table.shape[0] // lax.axis_size("reg")

    def disaggregate_onto(upper, lower):
        block = area_index_table
        total = jnp.einsum(
            "pr,pqh->rqh", block, lax.all_gather(upper, "reg", axis=0, tiled=True), precision=high
        )
        block = item_index_table
        return total + jnp.einsum(
            "crh,cq->rqh", lax.all_gather(lower, "prod", axis=0, tiled=True), block, precision=high
        )

    def replicate_across(corner):
        return jnp.einsum("pch,cq->pqh", corner, item_index_table, precision=high)

    def operate(field):
        rows_local = jnp.einsum("pr,rqh->pqh", area_index_table, field, precision=high)
        row_share = lax.psum_scatter(rows_local, "reg", scatter_dimension=0, tiled=True)
        col_share = lax.psum_scatter(
            jnp.einsum("cq,rqh->crh", item_index_table, field, precision=high),
            "prod",
            scatter_dimension=0,
            tiled=True,
        )
        partial_corner = jnp.einsum("pqh,cq->pch", rows_local, item_index_table, precision=high)
        whole = lax.psum(partial_corner, ("reg", "prod"))
        corner_share = lax.dynamic_slice_in_dim(
            whole, lax.axis_index("reg") * parent_share, parent_share, 0
        )
        upper = group_item_precision[:, :, None] * row_share + replicate_across(
            group_class_precision[:, :, None] * corner_share
        )
        lower = jnp.transpose(area_class_precision)[:, :, None] * col_share
        return bottom_series_precision[:, :, None] * field + disaggregate_onto(upper, lower)

    major_axis_first = group_item_precision[:, :, None] * group_item_predictions + replicate_across(
        group_class_precision[:, :, None] * group_class_predictions
    )
    lower_leading = jnp.transpose(
        area_class_precision[:, :, None] * area_class_predictions, (1, 0, 2)
    )
    system_source_term = bottom_series_precision[
        :, :, None
    ] * bottom_series_predictions + disaggregate_onto(major_axis_first, lower_leading)

    def two_products(vector, image):
        return lax.psum((jnp.sum(vector * vector), jnp.sum(vector * image)), ("reg", "prod"))

    solution_field = jnp.zeros_like(system_source_term)
    residual = system_source_term
    image = operate(residual)
    norm_now, product = two_products(residual, image)
    alpha = norm_now / product
    direction, along = (residual, image)
    for step in range(ITERATIONS):
        solution_field = solution_field + alpha * direction
        residual = residual - alpha * along
        if step + 1 < ITERATIONS:
            image = operate(residual)
            norm_next, product = two_products(residual, image)
            ratio = norm_next / norm_now
            alpha = norm_next / (product - ratio * norm_next / alpha)
            direction = residual + ratio * direction
            along = image + ratio * along
            norm_now = norm_next
    return (solution_field, residual)


def solution(mesh):
    return jax.shard_map(
        on_device,
        mesh=mesh,
        in_specs=(
            P("reg", "prod", None),
            P("reg", "prod", None),
            P("reg", "prod", None),
            P("reg", None, None),
            P("reg", "prod"),
            P("reg", "prod"),
            P("reg", "prod"),
            P("reg", None),
            P(),
            P(),
        ),
        out_specs=(P("reg", "prod", None), P("reg", "prod", None)),
        check_vma=False,
    )
```

profile of v0, /device:TPU:12, one launch (start us, length us, event | category | flops | bytes accessed | tf_op | source)
XLA Modules:
  0.0 496.7 jit_solution(14481580540045878076)
XLA Ops:
  10.1 1.3 fusion.5
  11.4 6.9 %all_gather.18 = f32[32,32,128]{2,1,0:T(8,128)S(1)} all-gather(f32[8,32,128]{2,1,0:T(8,128)S(1)} %fusion.5), channel_id=1, replica_groups=mesh['reg'=4,'prod'=8] {'reg'}, dimensions={0}, use_global_device_ids=true | all-gather | bytes 655360 | tf_op jit(solution)/shard_map/all_gather | solution.py:39
  18.4 29.1 %all_gather.19 = f32[32,32,128]{2,1,0:T(8,128)S(1)} all-gather(f32[4,32,128]{2,1,0:T(8,128)S(1)} %fusion.24), channel_id=1, replica_groups=mesh['reg'=4,'prod'=8] {'prod'}, dimensions={0}, use_global_device_ids=true | all-gather | bytes 589824 | tf_op jit(solution)/shard_map/all_gather | solution.py:43
  47.5 0.7 fusion.16
  48.2 0.7 compare_reduce_fusion.1
  48.9 1.3 fusion.2
  50.6 1.5 convolution_bitcast_fusion.1
  52.1 1.1 copy.80
  53.3 0.7 fusion.13
  54.1 1.1 copy.86
  55.2 129.7 %all-reduce.5.cloned.1.call-done = f32[32,32,128]{2,1,0:T(8,128)} async-done(((f32[32,32,128]{2,1,0:T(8,128)}), f32[32,32,128]{2,1,0:T(8,128)}) %all-reduce.5.cloned.1.call-update) | async-done | bytes 524304 | tf_op jit(solution)/shard_map/psum | solution.py:59
  184.9 1.3 fusion.4
  186.2 6.5 %all_gather.20 = f32[32,32,128]{2,1,0:T(8,128)S(1)} all-gather(f32[8,32,128]{2,1,0:T(8,128)S(1)} %fusion.4), channel_id=1, replica_groups=mesh['reg'=4,'prod'=8] {'reg'}, dimensions={0}, use_global_device_ids=true | all-gather | bytes 655360 | tf_op jit(solution)/shard_map/all_gather | solution.py:39
  192.7 0.9 broadcast_multiply_fusion.1
  193.6 28.7 %all_gather.21 = f32[32,32,128]{2,1,0:T(8,128)S(1)} all-gather(f32[4,32,128]{2,1,0:T(8,128)S(1)} %broadcast_multiply_fusion.1), channel_id=1, replica_groups=mesh['reg'=4,'prod'=8] {'prod'}, dimensions={0}, use_global_device_ids=true | all-gather | bytes 589824 | tf_op jit(solution)/shard_map/all_gather | solution.py:43
  222.3 0.7 fusion.11
  223.1 1.6 multiply_reduce_fusion.2
  224.7 43.1 %all-reduce.1 = (f32[]{:T(128)}, f32[]{:T(128)}) all-reduce(f32[]{:T(128)} %get-tuple-element.13, f32[]{:T(128)} %get-tuple-element.12), channel_id=1, replica_groups=mesh['reg'=4,'prod'=8] {'reg','prod'}, use_global_device_ids=true, to_apply=%region_3.0 | all-reduce | flops 2 | bytes 16 | tf_op jit(solution)/shard_map/psum | solution.py:80
  269.5 1.5 convolution_bitcast_fusion
  271.1 1.1 copy.90
  272.5 0.7 fusion.8
  273.2 1.1 copy.96
  274.3 125.1 %all-reduce.7.cloned.1.call-done = f32[32,32,128]{2,1,0:T(8,128)} async-done(((f32[32,32,128]{2,1,0:T(8,128)}), f32[32,32,128]{2,1,0:T(8,128)}) %all-reduce.7.cloned.1.call-update) | async-done | bytes 524304 | tf_op jit(solution)/shard_map/psum | solution.py:59
  399.4 1.3 fusion.3
  400.7 6.5 %all_gather.22 = f32[32,32,128]{2,1,0:T(8,128)S(1)} all-gather(f32[8,32,128]{2,1,0:T(8,128)S(1)} %fusion.3), channel_id=1, replica_groups=mesh['reg'=4,'prod'=8] {'reg'}, dimensions={0}, use_global_device_ids=true | all-gather | bytes 655360 | tf_op jit(solution)/shard_map/all_gather | solution.py:39
  407.2 0.9 broadcast_multiply_fusion
  408.1 28.8 %all_gather.23 = f32[32,32,128]{2,1,0:T(8,128)S(1)} all-gather(f32[4,32,128]{2,1,0:T(8,128)S(1)} %broadcast_multiply_fusion), channel_id=1, replica_groups=mesh['reg'=4,'prod'=8] {'prod'}, dimensions={0}, use_global_device_ids=true | all-gather | bytes 589824 | tf_op jit(solution)/shard_map/all_gather | solution.py:43
  436.9 0.7 fusion.6
  437.6 1.6 multiply_reduce_fusion
  439.2 42.9 %all-reduce = (f32[]{:T(128)}, f32[]{:T(128)}) all-reduce(f32[]{:T(128)} %get-tuple-element.11, f32[]{:T(128)} %get-tuple-element.10), channel_id=1, replica_groups=mesh['reg'=4,'prod'=8] {'reg','prod'}, use_global_device_ids=true, to_apply=%region_10.0 | all-reduce | flops 2 | bytes 16 | tf_op jit(solution)/shard_map/psum | solution.py:80
  486.9 1.1 copy.101
  488.0 1.1 copy.100
  (41 shorter events, 3.8 us)
Async XLA Ops:
  8.0 0.7 copy-start.5
  8.0 176.9 %all-reduce.5.cloned.1.call-start = ((), (), s32[]{:S(2)}) async-start(), calls=%async_computation.5 | async-start | bytes 1048576 | tf_op jit(solution)/shard_map/psum | solution.py:59
  8.7 0.7 copy-start.6
  9.4 0.7 copy-start.2
  9.4 0.7 copy-start.3
  11.4 6.9 %copy-start.1 = (f32[32,4,128]{2,1,0:T(4,128)S(1)}, f32[32,4,128]{2,1,0:T(4,128)}, u32[]{:S(2)}) copy-start(f32[32,4,128]{2,1,0:T(4,128)} %param.12) | copy-start | bytes 196612
  11.4 6.9 %copy-start.4 = (f32[32,4]{0,1:T(4,128)S(1)}, f32[32,4]{0,1:T(4,128)}, u32[]{:S(2)}) copy-start(f32[32,4]{0,1:T(4,128)} %param.16) | copy-start | bytes 1540
  47.5 0.7 copy-start.7
  47.5 1.4 copy-start
  52.1 132.8 %reduce-scatter.5.cloned.1.call-start = ((), (), s32[]{:S(2)}) async-start(), calls=%async_computation.4 | async-start | bytes 655360 | tf_op jit(solution)/shard_map/reduce_scatter | solution.py:51
  53.3 139.4 %reduce-scatter.7.cloned.1.call-start = ((), (), s32[]{:S(2)}) async-start(), calls=%async_computation.6 | async-start | bytes 589824 | tf_op jit(solution)/shard_map/reduce_scatter | solution.py:52
  55.2 344.2 %all-reduce.7.cloned.1.call-start = ((), (), s32[]{:S(2)}) async-start(), calls=%async_computation.8 | async-start | bytes 1048576 | tf_op jit(solution)/shard_map/psum | solution.py:59
  271.0 128.4 %reduce-scatter.9.cloned.1.call-start = ((), (), s32[]{:S(2)}) async-start(), calls=%async_computation.7 | async-start | bytes 655360 | tf_op jit(solution)/shard_map/reduce_scatter | solution.py:51
  272.2 134.9 %reduce-scatter.11.cloned.1.call-start = ((), (), s32[]{:S(2)}) async-start(), calls=%async_computation.9 | async-start | bytes 589824 | tf_op jit(solution)/shard_map/reduce_scatter | solution.py:52
Sparse Core Ops, SparseCore 0:
  52.2 132.6 all-reduce.4
  271.2 128.1 all-reduce.6
Sparse Core Ops, SparseCore 1:
  55.1 24.1 reduce-scatter.4
  83.0 63.4 reduce-scatter.6
  274.0 19.7 reduce-scatter.8
  297.7 63.5 reduce-scatter.10
where the time goes:
time: 498 us; the launch traced here: 497 us
  waiting for transfers between devices  255 us (51%)
  blocking collectives  192 us (39%)
  between operations  21.7 us (4%)
  matrix products  15.5 us (3%)
  local copies, waits for them, and re-layouts  8.02 us (2%)
    psum x2, waiting for transfers between devices, operate(): whole = lax.psum(partial_corner, ('reg', 'prod'))  255 us
    all_gather x3, blocking collectives, disaggregate_onto(): lax.all_gather(lower, 'prod', axis=0, tiled=True)  86.6 us
    psum x2, blocking collectives, two_products(): lax.psum((jnp.sum(vector * vector), jnp.sum(vector * image)), ('reg', 'pr...  86 us
    all_gather x3, blocking collectives, disaggregate_onto(): lax.all_gather(upper, 'reg', axis=0, tiled=True)  19.9 us
  transfers between devices with their start and end apart: 6, of which 2 were waited for; matrix products, arithmetic and copies ran while one was open for 2% of the time, Pallas kernels for 0%

commit v1 on v0

--- a/solution.py
+++ b/solution.py
@@ -4,6 +4,18 @@
 from jax.sharding import PartitionSpec as P
 
 ITERATIONS = 2
+
+
+def summed_around(array, axis, dim, contribution):
+    size, index, width = (lax.axis_size(axis), lax.axis_index(axis), array.shape[dim])
+    upward = [(i, (i + 1) % size) for i in range(size)]
+    held, total = (array, None)
+    for step in range(size):
+        coming = lax.ppermute(held, axis, upward) if step < size - 1 else None
+        absorb = contribution(held, (index - step) % size * width)
+        total = absorb if total is None else total + absorb
+        held = coming
+    return total
 
 
 def member_local(table, first, count):
@@ -39,8 +51,16 @@
             "pr,pqh->rqh", block, lax.all_gather(upper, "reg", axis=0, tiled=True), precision=high
         )
         block = item_index_table
-        return total + jnp.einsum(
-            "crh,cq->rqh", lax.all_gather(lower, "prod", axis=0, tiled=True), block, precision=high
+        return total + summed_around(
+            lower,
+            "prod",
+            0,
+            lambda own_block, at: jnp.einsum(
+                "crh,cq->rqh",
+                own_block,
+                lax.dynamic_slice_in_dim(block, at, own_block.shape[0], axis=0),
+                precision=high,
+            ),
         )
 
     def replicate_across(corner):

time: 498 us -> 541 us (1.086)
  waiting for transfers between devices: 255 us -> 350 us
  blocking collectives: 192 us -> 115 us
  matrix products: 15.5 us -> 30.1 us
  starting transfers between devices: 0.44 us -> 10.5 us
    reduce_scatter x2, waiting for transfers between devices: 0.01 us -> 122 us  [operate(): lax.psum_scatter(jnp.einsum('cq,rqh->crh', item_index_table, field, preci...]
    psum x2, waiting for transfers between devices: 255 us -> 138 us  [operate(): whole = lax.psum(partial_corner, ('reg', 'prod'))]
    ppermute x0 -> x21, waiting for transfers between devices: none -> 89.8 us  [summed_around(): coming = lax.ppermute(held, axis, upward) if step < size - 1 else None]
    all_gather x3 -> x0, blocking collectives: 86.6 us -> none  [disaggregate_onto(): lax.all_gather(lower, 'prod', axis=0, tiled=True)]
    ppermute x0 -> x21, starting transfers between devices: none -> 10.2 us  [summed_around(): coming = lax.ppermute(held, axis, upward) if step < size - 1 else None]
    psum x2, blocking collectives: 86 us -> 95.1 us  [two_products(): lax.psum((jnp.sum(vector * vector), jnp.sum(vector * image)), ('reg', 'pr...]
    dot_general x3 -> x24, matrix products: 2.14 us -> 10.6 us  [disaggregate_onto(): jnp.einsum('crh,cq->rqh', own_block, lax.dynamic_slice_in_dim(block, at,...]
    dot_general x3, matrix products: 4.43 us -> 11.5 us  [disaggregate_onto(): jnp.einsum('pr,pqh->rqh', block, lax.all_gather(upper, 'reg', axis=0, til...]
  transfers between devices with their start and end apart: 6 -> 27, of which waited for: 2 -> 22; matrix products, arithmetic and copies ran while one was open for 2% -> 4% of each run, Pallas kernels for 0% -> 0%
where the time goes in v1:
time: 541 us; the launch traced here: 540 us
  waiting for transfers between devices  350 us (65%)
  blocking collectives  115 us (21%)
  matrix products  30.1 us (6%)
  between operations  21.7 us (4%)
  starting transfers between devices  10.5 us (2%)
  local copies, waits for them, and re-layouts  8.96 us (2%)
    psum x2, waiting for transfers between devices, operate(): whole = lax.psum(partial_corner, ('reg', 'prod'))  138 us
    reduce_scatter x2, waiting for transfers between devices, operate(): lax.psum_scatter(jnp.einsum('cq,rqh->crh', item_index_table, field, preci...  122 us
    psum x2, blocking collectives, two_products(): lax.psum((jnp.sum(vector * vector), jnp.sum(vector * image)), ('reg', 'pr...  95.1 us
    ppermute x21, waiting for transfers between devices, summed_around(): coming = lax.ppermute(held, axis, upward) if step < size - 1 else None  89.8 us
    all_gather x3, blocking collectives, disaggregate_onto(): lax.all_gather(upper, 'reg', axis=0, tiled=True)  19.5 us
    dot_general x3, matrix products, disaggregate_onto(): jnp.einsum('pr,pqh->rqh', block, lax.all_gather(upper, 'reg', axis=0, til...  11.5 us
  transfers between devices with their start and end apart: 27, of which 22 were waited for; matrix products, arithmetic and copies ran while one was open for 4% of the time, Pallas kernels for 0%

profile of v1, /device:TPU:12, one launch (start us, length us, event | category | flops | bytes accessed | tf_op | source)
XLA Modules:
  0.0 540.3 jit_solution(8463734892457041524)
XLA Ops:
  13.1 6.5 %all_gather.9 = f32[32,32,128]{2,1,0:T(8,128)S(1)} all-gather(f32[8,32,128]{2,1,0:T(8,128)S(1)} %fusion.2), channel_id=1, replica_groups=mesh['reg'=4,'prod'=8] {'reg'}, dimensions={0}, use_global_device_ids=true | all-gather | bytes 655360 | tf_op jit(solution)/shard_map/all_gather | solution.py:51
  21.1 1.6 collective-permute-start.1
  23.1 3.2 collective-permute-done.1
  27.5 4.1 collective-permute-done.2
  32.0 4.7 collective-permute-done.3
  37.1 4.7 collective-permute-done.4
  42.4 6.0 %collective-permute-done.5 = f32[4,32,128]{2,0,1:T(4,128)S(1)} collective-permute-done((f32[4,32,128]{2,0,1:T(4,128)S(1)}, f32[4,32,128]{2,0,1:T(4,128)S(1)}, u32[]{:S(2)}, u32[]{:S(2)}) %collective-permute-start.5) | collective-permute-done | bytes 65568 | tf_op jit(solution)/shard_map/ppermute | solution.py:14
  48.9 6.5 %collective-permute-done.6 = f32[4,32,128]{2,0,1:T(4,128)S(1)} collective-permute-done((f32[4,32,128]{2,0,1:T(4,128)S(1)}, f32[4,32,128]{2,0,1:T(4,128)S(1)}, u32[]{:S(2)}, u32[]{:S(2)}) %collective-permute-start.6) | collective-permute-done | bytes 65568 | tf_op jit(solution)/shard_map/ppermute | solution.py:14
  55.9 3.7 fusion.5
  65.4 63.5 %reduce-scatter.7.cloned.1.call-done = f32[4,32,128]{2,1,0:T(8,128)} async-done(((f32[32,32,128]{2,1,0:T(8,128)}), f32[4,32,128]{2,1,0:T(8,128)}) %reduce-scatter.7.cloned.1.call-update) | async-done | bytes 65552 | tf_op jit(solution)/shard_map/reduce_scatter | solution.py:72
  129.8 1.7 collective-permute-start.7
  132.0 69.1 %all-reduce.5.cloned.1.call-done = f32[32,32,128]{2,1,0:T(8,128)} async-done(((f32[32,32,128]{2,1,0:T(8,128)}), f32[32,32,128]{2,1,0:T(8,128)}) %all-reduce.5.cloned.1.call-update) | async-done | bytes 524304 | tf_op jit(solution)/shard_map/psum | solution.py:79
  202.3 6.5 %all_gather.10 = f32[32,32,128]{2,1,0:T(8,128)S(1)} all-gather(f32[8,32,128]{2,1,0:T(8,128)S(1)} %fusion.1), channel_id=1, replica_groups=mesh['reg'=4,'prod'=8] {'reg'}, dimensions={0}, use_global_device_ids=true | all-gather | bytes 655360 | tf_op jit(solution)/shard_map/all_gather | solution.py:51
  210.5 3.6 collective-permute-done.8
  214.8 4.4 collective-permute-done.9
  219.7 4.7 collective-permute-done.10
  224.9 4.7 collective-permute-done.11
  230.0 6.3 %collective-permute-done.12 = f32[4,32,128]{2,0,1:T(4,128)S(1)} collective-permute-done((f32[4,32,128]{2,0,1:T(4,128)S(1)}, f32[4,32,128]{2,0,1:T(4,128)S(1)}, u32[]{:S(2)}, u32[]{:S(2)}) %collective-permute-start.12) | collective-permute-done | bytes 65568 | tf_op jit(solution)/shard_map/ppermute | solution.py:14
  236.8 6.5 %collective-permute-done.13 = f32[4,32,128]{2,0,1:T(4,128)S(1)} collective-permute-done((f32[4,32,128]{2,0,1:T(4,128)S(1)}, f32[4,32,128]{2,0,1:T(4,128)S(1)}, u32[]{:S(2)}, u32[]{:S(2)}) %collective-permute-start.13) | collective-permute-done | bytes 65568 | tf_op jit(solution)/shard_map/ppermute | solution.py:14
  243.8 3.9 multiply_reduce_fusion.2
  247.7 47.6 %all-reduce.1 = (f32[]{:T(128)}, f32[]{:T(128)}) all-reduce(f32[]{:T(128)} %get-tuple-element.13, f32[]{:T(128)} %get-tuple-element.12), channel_id=1, replica_groups=mesh['reg'=4,'prod'=8] {'reg','prod'}, use_global_device_ids=true, to_apply=%region_3.4 | all-reduce | flops 2 | bytes 16 | tf_op jit(solution)/shard_map/psum | solution.py:100
  301.6 58.2 %reduce-scatter.11.cloned.1.call-done = f32[4,32,128]{2,1,0:T(8,128)} async-done(((f32[32,32,128]{2,1,0:T(8,128)}), f32[4,32,128]{2,1,0:T(8,128)}) %reduce-scatter.11.cloned.1.call-update) | async-done | bytes 65552 | tf_op jit(solution)/shard_map/reduce_scatter | solution.py:72
  362.7 69.3 %all-reduce.7.cloned.1.call-done = f32[32,32,128]{2,1,0:T(8,128)} async-done(((f32[32,32,128]{2,1,0:T(8,128)}), f32[32,32,128]{2,1,0:T(8,128)}) %all-reduce.7.cloned.1.call-update) | async-done | bytes 524304 | tf_op jit(solution)/shard_map/psum | solution.py:79
  433.2 6.5 %all_gather.11 = f32[32,32,128]{2,1,0:T(8,128)S(1)} all-gather(f32[8,32,128]{2,1,0:T(8,128)S(1)} %fusion), channel_id=1, replica_groups=mesh['reg'=4,'prod'=8] {'reg'}, dimensions={0}, use_global_device_ids=true | all-gather | bytes 655360 | tf_op jit(solution)/shard_map/all_gather | solution.py:51
  441.4 3.6 collective-permute-done.15
  445.8 4.4 collective-permute-done.16
  450.6 4.7 collective-permute-done.17
  455.8 4.7 collective-permute-done.18
  460.9 6.3 %collective-permute-done.19 = f32[4,32,128]{2,0,1:T(4,128)S(1)} collective-permute-done((f32[4,32,128]{2,0,1:T(4,128)S(1)}, f32[4,32,128]{2,0,1:T(4,128)S(1)}, u32[]{:S(2)}, u32[]{:S(2)}) %collective-permute-start.19) | collective-permute-done | bytes 65568 | tf_op jit(solution)/shard_map/ppermute | solution.py:14
  467.7 6.5 %collective-permute-done.20 = f32[4,32,128]{2,0,1:T(4,128)S(1)} collective-permute-done((f32[4,32,128]{2,0,1:T(4,128)S(1)}, f32[4,32,128]{2,0,1:T(4,128)S(1)}, u32[]{:S(2)}, u32[]{:S(2)}) %collective-permute-start.20) | collective-permute-done | bytes 65568 | tf_op jit(solution)/shard_map/ppermute | solution.py:14
  474.7 3.9 multiply_reduce_fusion
  478.6 47.5 %all-reduce = (f32[]{:T(128)}, f32[]{:T(128)}) all-reduce(f32[]{:T(128)} %get-tuple-element.11, f32[]{:T(128)} %get-tuple-element.10), channel_id=1, replica_groups=mesh['reg'=4,'prod'=8] {'reg','prod'}, use_global_device_ids=true, to_apply=%region_10.11 | all-reduce | flops 2 | bytes 16 | tf_op jit(solution)/shard_map/psum | solution.py:100
  (105 shorter events, 39.3 us)
Async XLA Ops:
  8.0 120.9 %reduce-scatter.7.cloned.1.call-start = ((), (), s32[]{:S(2)}) async-start(), calls=%async_computation.6 | async-start | bytes 589824 | tf_op jit(solution)/shard_map/reduce_scatter | solution.py:72
  9.7 11.3 %collective-permute-start = (f32[4,32,128]{2,0,1:T(4,128)S(1)}, f32[4,32,128]{2,0,1:T(4,128)S(1)}, u32[]{:S(2)}, u32[]{:S(2)}) collective-permute-start(f32[4,32,128]{2,0,1:T(4,128)S(1)} %multiply_bitcast_fusion), channel_id=1, source_target_pairs={{0,1},{1,2},{2,3},{3,4},{4,5},{5,6},{6,7},{7,0},{8,9},{9,10},{10,1... | collective-permute-start | bytes 196616 | tf_op jit(solution)/shard_map/ppermute | solution.py:14
  11.3 1.5 copy-start.3
  11.3 1.5 copy-start.4
  11.3 1.5 copy-start.2
  11.3 1.5 copy-start.1
  21.1 5.3 collective-permute-start.1
  26.4 5.2 collective-permute-start.2
  31.5 5.2 collective-permute-start.3
  36.7 5.2 collective-permute-start.4
  41.9 6.6 %collective-permute-start.5 = (f32[4,32,128]{2,0,1:T(4,128)S(1)}, f32[4,32,128]{2,0,1:T(4,128)S(1)}, u32[]{:S(2)}, u32[]{:S(2)}) collective-permute-start(f32[4,32,128]{2,0,1:T(4,128)S(1)} %collective-permute-done.4), channel_id=1, source_target_pairs={{0,1},{1,2},{2,3},{3,4},{4,5},{5,6},{6,7},{7,0},{8,9},{9,10},{10,1... | collective-permute-start | bytes 196616 | tf_op jit(solution)/shard_map/ppermute | solution.py:14
  42.4 13.5 %copy-start = (f32[32,32,128]{2,1,0:T(8,128)S(1)}, f32[32,32,128]{2,1,0:T(8,128)}, u32[]{:S(2)}) copy-start(f32[32,32,128]{2,1,0:T(8,128)} %param.10) | copy-start | bytes 1572868
  48.5 7.0 %collective-permute-start.6 = (f32[4,32,128]{2,0,1:T(4,128)S(1)}, f32[4,32,128]{2,0,1:T(4,128)S(1)}, u32[]{:S(2)}, u32[]{:S(2)}) collective-permute-start(f32[4,32,128]{2,0,1:T(4,128)S(1)} %collective-permute-done.5), channel_id=1, source_target_pairs={{0,1},{1,2},{2,3},{3,4},{4,5},{5,6},{6,7},{7,0},{8,9},{9,10},{10,1... | collective-permute-start | bytes 196616 | tf_op jit(solution)/shard_map/ppermute | solution.py:14
  61.5 139.6 %all-reduce.5.cloned.1.call-start = ((), (), s32[]{:S(2)}) async-start(), calls=%async_computation.5 | async-start | bytes 1048576 | tf_op jit(solution)/shard_map/psum | solution.py:79
  63.4 137.6 %reduce-scatter.5.cloned.1.call-start = ((), (), s32[]{:S(2)}) async-start(), calls=%async_computation.4 | async-start | bytes 655360 | tf_op jit(solution)/shard_map/reduce_scatter | solution.py:71
  64.6 295.2 %reduce-scatter.11.cloned.1.call-start = ((), (), s32[]{:S(2)}) async-start(), calls=%async_computation.9 | async-start | bytes 589824 | tf_op jit(solution)/shard_map/reduce_scatter | solution.py:72
  129.8 79.0 %collective-permute-start.7 = (f32[4,32,128]{2,0,1:T(4,128)S(1)}, f32[4,32,128]{2,0,1:T(4,128)S(1)}, u32[]{:S(2)}, u32[]{:S(2)}) collective-permute-start(f32[4,32,128]{2,0,1:T(4,128)S(1)} %copy_multiply_fusion.2), channel_id=1, source_target_pairs={{0,1},{1,2},{2,3},{3,4},{4,5},{5,6},{6,7},{7,0},{8,9},{9,10},{10,1... | collective-permute-start | bytes 196616 | tf_op jit(solution)/shard_map/ppermute | solution.py:14
  208.8 5.2 collective-permute-start.8
  214.1 5.2 collective-permute-start.9
  219.2 5.2 collective-permute-start.10
  224.4 5.2 collective-permute-start.11
  229.6 6.8 %collective-permute-start.12 = (f32[4,32,128]{2,0,1:T(4,128)S(1)}, f32[4,32,128]{2,0,1:T(4,128)S(1)}, u32[]{:S(2)}, u32[]{:S(2)}) collective-permute-start(f32[4,32,128]{2,0,1:T(4,128)S(1)} %collective-permute-done.11), channel_id=1, source_target_pairs={{0,1},{1,2},{2,3},{3,4},{4,5},{5,6},{6,7},{7,0},{8,9},{9,10},{10,1... | collective-permute-start | bytes 196616 | tf_op jit(solution)/shard_map/ppermute | solution.py:14
  236.3 7.0 %collective-permute-start.13 = (f32[4,32,128]{2,0,1:T(4,128)S(1)}, f32[4,32,128]{2,0,1:T(4,128)S(1)}, u32[]{:S(2)}, u32[]{:S(2)}) collective-permute-start(f32[4,32,128]{2,0,1:T(4,128)S(1)} %collective-permute-done.12), channel_id=1, source_target_pairs={{0,1},{1,2},{2,3},{3,4},{4,5},{5,6},{6,7},{7,0},{8,9},{9,10},{10,1... | collective-permute-start | bytes 196616 | tf_op jit(solution)/shard_map/ppermute | solution.py:14
  298.5 133.5 %all-reduce.7.cloned.1.call-start = ((), (), s32[]{:S(2)}) async-start(), calls=%async_computation.8 | async-start | bytes 1048576 | tf_op jit(solution)/shard_map/psum | solution.py:79
  300.5 131.5 %reduce-scatter.9.cloned.1.call-start = ((), (), s32[]{:S(2)}) async-start(), calls=%async_computation.7 | async-start | bytes 655360 | tf_op jit(solution)/shard_map/reduce_scatter | solution.py:71
  360.8 79.0 %collective-permute-start.14 = (f32[4,32,128]{2,0,1:T(4,128)S(1)}, f32[4,32,128]{2,0,1:T(4,128)S(1)}, u32[]{:S(2)}, u32[]{:S(2)}) collective-permute-start(f32[4,32,128]{2,0,1:T(4,128)S(1)} %copy_multiply_fusion.1), channel_id=1, source_target_pairs={{0,1},{1,2},{2,3},{3,4},{4,5},{5,6},{6,7},{7,0},{8,9},{9,10},{10,1... | collective-permute-start | bytes 196616 | tf_op jit(solution)/shard_map/ppermute | solution.py:14
  439.7 5.2 collective-permute-start.15
  445.0 5.2 collective-permute-start.16
  450.2 5.2 collective-permute-start.17
  455.3 5.2 collective-permute-start.18
  460.5 6.8 %collective-permute-start.19 = (f32[4,32,128]{2,0,1:T(4,128)S(1)}, f32[4,32,128]{2,0,1:T(4,128)S(1)}, u32[]{:S(2)}, u32[]{:S(2)}) collective-permute-start(f32[4,32,128]{2,0,1:T(4,128)S(1)} %collective-permute-done.18), channel_id=1, source_target_pairs={{0,1},{1,2},{2,3},{3,4},{4,5},{5,6},{6,7},{7,0},{8,9},{9,10},{10,1... | collective-permute-start | bytes 196616 | tf_op jit(solution)/shard_map/ppermute | solution.py:14
  467.3 7.0 %collective-permute-start.20 = (f32[4,32,128]{2,0,1:T(4,128)S(1)}, f32[4,32,128]{2,0,1:T(4,128)S(1)}, u32[]{:S(2)}, u32[]{:S(2)}) collective-permute-start(f32[4,32,128]{2,0,1:T(4,128)S(1)} %collective-permute-done.19), channel_id=1, source_target_pairs={{0,1},{1,2},{2,3},{3,4},{4,5},{5,6},{6,7},{7,0},{8,9},{9,10},{10,1... | collective-permute-start | bytes 196616 | tf_op jit(solution)/shard_map/ppermute | solution.py:14
  (4 other events, 2.9 us)
Sparse Core Ops, SparseCore 0:
  61.6 67.2 reduce-scatter.6
  131.4 19.8 reduce-scatter.4
  298.6 61.1 reduce-scatter.10
  362.2 19.8 reduce-scatter.8
Sparse Core Ops, SparseCore 1:
  67.8 133.2 all-reduce.4
  304.9 127.1 all-reduce.6
